TPU v7x, 256 devices: a whole 4x4x8 slice. The times are simulated.
256 devices in a mesh: band: 16 (over z_hi, x), plane: 16 (over y, z_lo, core).
Axes of the slice: x: 4, y: 4, z: 8 (z_hi: 4, z_lo: 2; z = z_hi * 2 + z_lo), core: 2. Of those that a mesh axis runs over, the one named last changes fastest.
Arguments:
- orbitals: float32 [16, 112, 12544], P('band', 'plane'), may hold values from -6 to 6
Outputs:
- exchange_w: float32 [16, 112, 12544], P('band', 'plane')
All inputs are finite; a program needn't handle non-finite values.
Results may differ from a plain program's by a relative error of at most 0.000082.
Values sent between devices are 32-bit elements; how exact they have to be, the bound alone decides.
A program may use at most 64 MiB of HBM per device.

v0:
```python
import math

import jax
import jax.numpy as jnp
from jax import lax
from jax.sharding import PartitionSpec as P

ROUNDS = 2


screen_omega = 0.106
cell_length = 46.93
mixing = 0.25
highest = lax.Precision.HIGHEST


def padded_to(lines, count):
    spare = -len(lines) % count
    return jnp.pad(lines, [(0, spare)] + [(0, 0)] * (lines.ndim - 1))


def laid_out(pieces, dim):
    pieces = jnp.moveaxis(pieces, 0, dim)
    shape = pieces.shape
    return pieces.reshape(*shape[:dim], shape[dim] * shape[dim + 1], *shape[dim + 2 :])


def sent_to_all(array, axis):
    count = lax.axis_size(axis)
    return lax.all_to_all(
        jnp.broadcast_to(array[None], (count, *array.shape)), axis, 0, 0, tiled=True
    )


def collect(array, axis, dim):
    return laid_out(sent_to_all(array, axis), dim)


def split_up(array, dim, count):
    before, after = (array.shape[:dim], array.shape[dim + 1 :])
    return jnp.moveaxis(array.reshape(*before, count, -1, *after), dim, 0)


def summed_on_arrival(array, axis, dim):
    count = lax.axis_size(axis)
    pieces = lax.all_to_all(split_up(array, dim, count), axis, 0, 0, tiled=True)
    return jnp.sum(pieces, axis=0)


def nested_sum(array, axes):
    lines = array.reshape(-1)
    padded = padded_to(lines, lax.axis_size(axes))
    whole = collect(summed_on_arrival(padded, axes, 0), axes, 0)
    return lax.slice_in_dim(whole, 0, len(lines)).reshape(array.shape)


def wave_number(index, count):
    return jnp.where(2 * index < count, index, index - count)


def kernel_values(squares):
    gsquare = squares * (2.0 * math.pi / cell_length) ** 2
    safe = jnp.where(gsquare > 0, gsquare, 1.0)
    values = 4.0 * math.pi / safe * (1.0 - jnp.exp(-safe / (4.0 * screen_omega * screen_omega)))
    return jnp.where(gsquare > 0, values, math.pi / (screen_omega * screen_omega))


def dft_tables(count):
    index = jnp.arange(count, dtype=jnp.int32)
    phase = index[:, None] * index[None, :] % count
    angle = phase.astype(jnp.float32) * (2.0 * math.pi / count)
    return (jnp.cos(angle), jnp.sin(angle))


def along_first(values, table):
    return jnp.einsum("pxyz,xk->pkyz", values, table, precision=highest)


def along_second(values, table):
    return jnp.einsum("pxyz,yk->pxkz", values, table, precision=highest)


def along_last(values, table):
    shape = values.shape
    flat = values.reshape(-1, shape[-1])
    return jnp.dot(flat, table, precision=highest, preferred_element_type=jnp.float32).reshape(
        shape
    )


def source_groups(orbitals):
    mine = lax.axis_index("band")
    slots = jnp.stack(
        [jnp.where(mine == root, orbitals, jnp.zeros_like(orbitals)) for root in range(ROUNDS)],
        axis=0,
    )
    shared = nested_sum(slots, "band")
    return [shared[root] for root in range(ROUNDS)]


def on_device(orbitals):
    nplane = lax.axis_size("plane")
    rows, thick, flat = orbitals.shape
    count = thick * nplane
    span = count // nplane
    cosine, sine = dft_tables(count)
    local = orbitals.reshape(rows, thick, count, count)
    start = lax.axis_index("plane") * span
    freq_all = wave_number(jnp.arange(count, dtype=jnp.int32), count).astype(jnp.float32)
    freq_mine = wave_number(start + jnp.arange(span, dtype=jnp.int32), count).astype(jnp.float32)
    kernel = kernel_values(
        freq_all[:, None, None] ** 2 + freq_mine[None, :, None] ** 2 + freq_all[None, None, :] ** 2
    )
    scale = 1.0 / float(count) ** 3
    pieces = source_groups(orbitals)
    gathered = jnp.concatenate(pieces, axis=0)
    remote = gathered.reshape(gathered.shape[0], thick, count, count)
    many = remote.shape[0]
    pairs = rows * many
    density = (local[:, None] * remote[None]).reshape(pairs, thick, count, count)
    half = (pairs + 1) // 2
    first_half = density[:half]
    second_half = density[half:]
    zed_real = along_last(first_half, cosine) + along_last(second_half, sine)
    zed_imag = along_last(second_half, cosine) - along_last(first_half, sine)
    why_real = along_second(zed_real, cosine) + along_second(zed_imag, sine)
    why_imag = along_second(zed_imag, cosine) - along_second(zed_real, sine)
    real_part = lax.all_to_all(why_real, "plane", split_axis=2, concat_axis=1, tiled=True)
    imag_part = lax.all_to_all(why_imag, "plane", split_axis=2, concat_axis=1, tiled=True)
    fwd_real = along_first(real_part, cosine) + along_first(imag_part, sine)
    fwd_imag = along_first(imag_part, cosine) - along_first(real_part, sine)
    fwd_real = fwd_real * kernel
    fwd_imag = fwd_imag * kernel
    inv_real = along_first(fwd_real, cosine) - along_first(fwd_imag, sine)
    inv_imag = along_first(fwd_real, sine) + along_first(fwd_imag, cosine)
    back_real = lax.all_to_all(inv_real, "plane", split_axis=1, concat_axis=2, tiled=True)
    back_imag = lax.all_to_all(inv_imag, "plane", split_axis=1, concat_axis=2, tiled=True)
    upper_real = along_second(back_real, cosine) - along_second(back_imag, sine)
    upper_imag = along_second(back_real, sine) + along_second(back_imag, cosine)
    first_pot = (along_last(upper_real, cosine) - along_last(upper_imag, sine)) * scale
    second_pot = (along_last(upper_real, sine) + along_last(upper_imag, cosine)) * scale
    potential = jnp.concatenate([first_pot, second_pot], axis=0)
    potential = potential.reshape(rows, many, thick, count, count)
    total = -mixing * jnp.sum(remote[None] * potential, axis=1)
    return total.reshape(rows, thick, flat)


def solution(mesh):
    placed = (P("band", "plane", None),)
    return jax.shard_map(
        on_device, mesh=mesh, in_specs=placed, out_specs=P("band", "plane", None), check_vma=False
    )
```

profile of v0, /device:TPU:1, one launch (start us, length us, event | category | flops | bytes accessed | tf_op | source)
XLA Modules:
  0.0 136.5 jit_solution(8775944873492629465)
XLA Ops:
  0.0 2.3 %fusion.228 = (f32[7,12544]{1,0:T(8,128)S(1)}, f32[1,1,7,12544]{3,0,2,1:T(1,128)S(1)}, f32[1,1,7,12544]{3,0,2,1:T(1,128)S(1)}) fusion(f32[1,7,12544]{2,0,1:T(1,128)} %param.1, pred[]{:T(512)S(6)} %eq.8, pred[]{:T(512)S(6)} %eq.9), kind=kLoop, calls=%fused_computation.214 | loop fusion | flops 175616 | bytes 1404930 | tf_op args[0]
  3.1 1.1 all_to_all.69
  4.2 30.9 %all_to_all.76 = f32[16,1,10976]{2,1,0:T(1,128)S(1)} all-to-all(f32[16,1,10976]{2,1,0:T(1,128)S(1)} %all_to_all.69), channel_id=1, replica_groups=mesh['band'=16,'plane'=16] {'band'}, dimensions={0} | all-to-all | bytes 1404928 | tf_op jit(solution)/shard_map/all_to_all | solution.py:46
  35.6 1.2 broadcast_in_dim.9
  36.8 5.7 %all-to-all-start.1 = ((f32[16,1,10976]{2,1,0:T(1,128)}), f32[16,1,10976]{2,1,0:T(1,128)S(1)}, u32[]{:S(2)}, u32[]{:S(2)}) async-start(f32[16,1,10976]{2,1,0:T(1,128)} %broadcast_in_dim.9), calls=%async_computation.1 | async-start | bytes 1409024 | tf_op jit(solution)/shard_map/all_to_all | solution.py:30
  42.8 19.3 %all-to-all-done.1 = f32[16,1,10976]{2,1,0:T(1,128)S(1)} async-done(((f32[16,1,10976]{2,1,0:T(1,128)}), f32[16,1,10976]{2,1,0:T(1,128)S(1)}, u32[]{:S(2)}, u32[]{:S(2)}) %all-to-all-start.1) | async-done | bytes 702496 | tf_op jit(solution)/shard_map/all_to_all | solution.py:30
  62.0 1.9 %slice_reduce_fusion = (f32[8,10976]{1,0:T(8,128)S(1)}, f32[8,10976]{1,0:T(8,128)S(1)}) fusion(f32[16,1,10976]{2,1,0:T(1,128)S(1)} %all-to-all-done.1), kind=kLoop, calls=%fused_computation.36 | loop fusion | bytes 1404928 | tf_op jit(solution)/shard_map/slice | solution.py:98
  68.1 0.8 fusion.4
  68.8 1.2 copy.83
  70.0 7.5 %all-to-all-start.3 = ((f32[1,7,112,112]{3,0,1,2:T(1,128)}), f32[1,7,112,112]{3,0,1,2:T(1,128)S(1)}, u32[]{:S(2)}, u32[]{:S(2)}) async-start(f32[1,7,112,112]{3,0,1,2:T(1,128)} %copy.83), calls=%async_computation.3 | async-start | bytes 802816 | tf_op jit(solution)/shard_map/all_to_all | solution.py:129
  79.0 1.2 copy.77
  80.2 5.7 %all-to-all-done.3 = f32[1,7,112,112]{3,0,1,2:T(1,128)S(1)} async-done(((f32[1,7,112,112]{3,0,1,2:T(1,128)}), f32[1,7,112,112]{3,0,1,2:T(1,128)S(1)}, u32[]{:S(2)}, u32[]{:S(2)}) %all-to-all-start.3) | async-done | bytes 351264 | tf_op jit(solution)/shard_map/all_to_all | solution.py:129
  85.8 4.6 %all-to-all-start.2 = ((f32[1,7,112,112]{3,0,1,2:T(1,128)}), f32[1,7,112,112]{3,0,1,2:T(1,128)S(1)}, u32[]{:S(2)}, u32[]{:S(2)}) async-start(f32[1,7,112,112]{3,0,1,2:T(1,128)} %copy.77), calls=%async_computation.2 | async-start | bytes 802816 | tf_op jit(solution)/shard_map/all_to_all | solution.py:128
  91.8 7.1 %all-to-all-done.2 = f32[1,7,112,112]{3,0,1,2:T(1,128)S(1)} async-done(((f32[1,7,112,112]{3,0,1,2:T(1,128)}), f32[1,7,112,112]{3,0,1,2:T(1,128)S(1)}, u32[]{:S(2)}, u32[]{:S(2)}) %all-to-all-start.2) | async-done | bytes 351264 | tf_op jit(solution)/shard_map/all_to_all | solution.py:128
  100.1 0.8 fusion.7
  101.0 0.8 fusion.6
  103.3 1.2 copy.91
  104.5 4.6 %all-to-all-start.4 = ((f32[1,112,7,112]{3,0,2,1:T(1,128)}), f32[1,112,7,112]{3,0,2,1:T(1,128)S(1)}, u32[]{:S(2)}, u32[]{:S(2)}) async-start(f32[1,112,7,112]{3,0,2,1:T(1,128)} %copy.91), calls=%async_computation.4 | async-start | bytes 802816 | tf_op jit(solution)/shard_map/all_to_all | solution.py:136
  110.6 1.2 copy.96
  111.7 5.8 %all-to-all-done.4 = f32[1,112,7,112]{3,0,2,1:T(1,128)S(1)} async-done(((f32[1,112,7,112]{3,0,2,1:T(1,128)}), f32[1,112,7,112]{3,0,2,1:T(1,128)S(1)}, u32[]{:S(2)}, u32[]{:S(2)}) %all-to-all-start.4) | async-done | bytes 351264 | tf_op jit(solution)/shard_map/all_to_all | solution.py:136
  117.5 4.6 %all-to-all-start.5 = ((f32[1,112,7,112]{3,0,2,1:T(1,128)}), f32[1,112,7,112]{3,0,2,1:T(1,128)S(1)}, u32[]{:S(2)}, u32[]{:S(2)}) async-start(f32[1,112,7,112]{3,0,2,1:T(1,128)} %copy.96), calls=%async_computation.5 | async-start | bytes 802816 | tf_op jit(solution)/shard_map/all_to_all | solution.py:137
  123.7 6.8 %all-to-all-done.5 = f32[1,112,7,112]{3,0,2,1:T(1,128)S(1)} async-done(((f32[1,112,7,112]{3,0,2,1:T(1,128)}), f32[1,112,7,112]{3,0,2,1:T(1,128)S(1)}, u32[]{:S(2)}, u32[]{:S(2)}) %all-to-all-start.5) | async-done | bytes 351264 | tf_op jit(solution)/shard_map/all_to_all | solution.py:137
  130.6 0.8 fusion.1
  135.2 1.3 mul.323
  (44 shorter events, 17.9 us)
Async XLA Ops:
  36.8 25.3 %all-to-all-start.1 = ((f32[16,1,10976]{2,1,0:T(1,128)}), f32[16,1,10976]{2,1,0:T(1,128)S(1)}, u32[]{:S(2)}, u32[]{:S(2)}) async-start(f32[16,1,10976]{2,1,0:T(1,128)} %broadcast_in_dim.9), calls=%async_computation.1 | async-start | bytes 1409024 | tf_op jit(solution)/shard_map/all_to_all | solution.py:30
  70.0 15.9 %all-to-all-start.3 = ((f32[1,7,112,112]{3,0,1,2:T(1,128)}), f32[1,7,112,112]{3,0,1,2:T(1,128)S(1)}, u32[]{:S(2)}, u32[]{:S(2)}) async-start(f32[1,7,112,112]{3,0,1,2:T(1,128)} %copy.83), calls=%async_computation.3 | async-start | bytes 802816 | tf_op jit(solution)/shard_map/all_to_all | solution.py:129
  85.8 13.0 %all-to-all-start.2 = ((f32[1,7,112,112]{3,0,1,2:T(1,128)}), f32[1,7,112,112]{3,0,1,2:T(1,128)S(1)}, u32[]{:S(2)}, u32[]{:S(2)}) async-start(f32[1,7,112,112]{3,0,1,2:T(1,128)} %copy.77), calls=%async_computation.2 | async-start | bytes 802816 | tf_op jit(solution)/shard_map/all_to_all | solution.py:128
  104.5 13.0 %all-to-all-start.4 = ((f32[1,112,7,112]{3,0,2,1:T(1,128)}), f32[1,112,7,112]{3,0,2,1:T(1,128)S(1)}, u32[]{:S(2)}, u32[]{:S(2)}) async-start(f32[1,112,7,112]{3,0,2,1:T(1,128)} %copy.91), calls=%async_computation.4 | async-start | bytes 802816 | tf_op jit(solution)/shard_map/all_to_all | solution.py:136
  117.5 13.0 %all-to-all-start.5 = ((f32[1,112,7,112]{3,0,2,1:T(1,128)}), f32[1,112,7,112]{3,0,2,1:T(1,128)S(1)}, u32[]{:S(2)}, u32[]{:S(2)}) async-start(f32[1,112,7,112]{3,0,2,1:T(1,128)} %copy.96), calls=%async_computation.5 | async-start | bytes 802816 | tf_op jit(solution)/shard_map/all_to_all | solution.py:137
where the time goes:
time: 137 us
  waiting for transfers between devices  44.7 us (33%)
  blocking collectives  30.9 us (23%)
  starting transfers between devices  27 us (20%)
  matrix products  17.8 us (13%)
  local copies, waits for them, and re-layouts  12 us (9%)
  other arithmetic  3.73 us (3%)
    all_to_all x1, blocking collectives, summed_on_arrival(): pieces = lax.all_to_all(split_up(array, dim, count), axis, 0, 0, tiled=True)  30.9 us
    all_to_all x1, waiting for transfers between devices, sent_to_all(): lax.all_to_all(jnp.broadcast_to(array[None], (count, *array.shape)), axis...  19.3 us
    all_to_all x1, starting transfers between devices, on_device(): lax.all_to_all(why_imag, 'plane', split_axis=2, concat_axis=1, tiled=True)  7.51 us
    all_to_all x1, waiting for transfers between devices, on_device(): lax.all_to_all(why_real, 'plane', split_axis=2, concat_axis=1, tiled=True)  7.1 us
    all_to_all x1, waiting for transfers between devices, on_device(): lax.all_to_all(inv_imag, 'plane', split_axis=1, concat_axis=2, tiled=True)  6.84 us
    dot_general x8, matrix products, along_first(): return jnp.einsum('pxyz,xk->pkyz', values, table, precision=highest)  6.14 us
    dot_general x8, matrix products, along_second(): return jnp.einsum('pxyz,yk->pxkz', values, table, precision=highest)  5.98 us
    all_to_all x1, waiting for transfers between devices, on_device(): lax.all_to_all(inv_real, 'plane', split_axis=1, concat_axis=2, tiled=True)  5.76 us
  transfers between devices with their start and end apart: 5, of which 5 were waited for; matrix products, arithmetic and copies ran while one was open for 6% of the time, Pallas kernels for 0%

commit v1 on v0

v1 whole, which is shorter than its diff:
```python
import functools
import math

import jax
import jax.numpy as jnp
import ml_dtypes
import numpy as np
from jax import lax
from jax.experimental import pallas as pl
from jax.experimental.pallas import tpu as pltpu
from jax.sharding import PartitionSpec as P

MESH = pl.DeviceIdType.MESH
NG = 112
FLAT = NG * NG
HALF = FLAT // 2
CHUNKS = ((0, 3200), (3200, 3072))
SHARES = 16
THICK = NG // SHARES
ROWS = 2 * THICK
BLOCK = 112
USED = THICK * ROWS
screen_omega = 0.106
cell_length = 46.93
mixing = 0.25
f32, bf16 = jnp.float32, jnp.bfloat16


def tables():
    index = np.arange(NG)
    angle = (index[:, None] * index[None, :] % NG) * (2.0 * math.pi / NG)
    cos, sin = np.cos(angle), np.sin(angle)
    re, im = slice(0, NG), slice(128, 128 + NG)
    last = np.zeros((256, 256))
    last[re, re], last[im, re] = cos, sin
    last[re, im], last[im, im] = -sin, cos
    last_back = np.zeros((256, 256))
    last_back[re, re], last_back[im, re] = cos, -sin
    last_back[re, im], last_back[im, im] = sin, cos
    second = np.zeros((256, 256))
    second_back = np.zeros((256, 256))
    for share in range(SHARES):
        for part in range(2):
            for k in range(THICK):
                row, wave = 16 * share + THICK * part + k, THICK * share + k
                if part == 0:
                    second[row, 0:NG], second[row, NG : 2 * NG] = cos[wave], sin[wave]
                    second_back[0:NG, row], second_back[NG : 2 * NG, row] = cos[wave], sin[wave]
                else:
                    second[row, 0:NG], second[row, NG : 2 * NG] = -sin[wave], cos[wave]
                    second_back[0:NG, row], second_back[NG : 2 * NG, row] = -sin[wave], cos[wave]
    place = 8 * (index // THICK) + index % THICK
    first = np.zeros((256, 256))
    first_back = np.zeros((256, 256))
    first[re, place], first[re, 128 + place] = cos, sin
    first[im, place], first[im, 128 + place] = -sin, cos
    first_back[place, re], first_back[place, im] = cos, -sin
    first_back[128 + place, re], first_back[128 + place, im] = sin, cos
    both = []
    for table in (last, second, first, first_back, second_back, last_back):
        high = table.astype(ml_dtypes.bfloat16)
        both += [high, (table - high.astype(np.float64)).astype(ml_dtypes.bfloat16)]
    return np.stack(both)


def split(values):
    high = values.astype(bf16)
    return high, (values - high.astype(f32)).astype(bf16)


def dot(a, b):
    return jnp.dot(a, b, preferred_element_type=f32)


def from_left(high, low, values):
    big, small = split(values)
    return dot(high, big) + dot(high, small) + dot(low, big)


def from_right(values, high, low):
    big, small = split(values)
    return dot(big, high) + dot(small, high) + dot(big, low)


def kernel_tile(k_second, shape):
    def wave(index):
        return jnp.where(2 * index < NG, index, index - NG).astype(f32)

    first = wave(lax.broadcasted_iota(jnp.int32, shape, 0))
    last = wave(lax.broadcasted_iota(jnp.int32, shape, 1))
    second = wave(jnp.full(shape, k_second, jnp.int32))
    gsquare = (first * first + second * second + last * last) * (2.0 * math.pi / cell_length) ** 2
    safe = jnp.where(gsquare > 0, gsquare, 1.0)
    values = 4.0 * math.pi / safe * (1.0 - jnp.exp(-safe / (4.0 * screen_omega * screen_omega)))
    values = jnp.where(gsquare > 0, values, math.pi / (screen_omega * screen_omega))
    return values * (-mixing / float(NG) ** 3)


def body(
    psi_hbm, tab_hbm, out,
    psi, tab, src, work, spec, kern, s_out, r_in, g_out, h_in, sums, srows,
    load_sem, zs, zr, xs, xr, fs, fr, bs, br,
):
    band, me = lax.axis_index("band"), lax.axis_index("plane")
    x, zh = band % 4, band // 4

    def at_x(d):
        return (zh * 4 + (x + d) % 4, me)

    def at_z(d):
        return (((zh + d) % 4) * 4 + x, me)

    def at_plane(d):
        return (band, (me + d) % SHARES)

    barrier = pltpu.get_barrier_semaphore()
    peers = [at_x(d) for d in (1, 2, 3)] + [at_z(1), at_z(3)] + [at_plane(d) for d in range(1, SHARES)]
    for peer in peers:
        pl.semaphore_signal(barrier, inc=1, device_id=peer, device_id_type=MESH)

    load_psi = pltpu.make_async_copy(psi_hbm, psi, load_sem.at[0])
    load_psi.start()
    load_tab = pltpu.make_async_copy(tab_hbm, tab, load_sem.at[1])
    load_tab.start()

    origin = jnp.logical_and(zh == 0, x < 2)

    def piece(which, chunk):
        start, length = CHUNKS[chunk]
        offset = pl.multiple_of((which // 2) * HALF + start, 128)
        return src.at[((which + 1) // 2) % 2, :, pl.ds(offset, length)]

    def own_load(chunk):
        start, length = CHUNKS[chunk]
        return pltpu.make_async_copy(
            psi_hbm.at[:, pl.ds(start, length)], piece(x, chunk), load_sem.at[2 + chunk]
        )

    @pl.when(origin)
    def _():
        for chunk in range(2):
            own_load(chunk).start()

    work[...] = jnp.zeros_like(work)
    for buffer in (s_out, r_in, h_in):
        for share in range(SHARES):
            rows = slice(BLOCK * share + USED, BLOCK * (share + 1))
            buffer[rows, :] = jnp.zeros((BLOCK - USED, 128), f32)
    srows[...] = jnp.zeros_like(srows)
    for k in range(THICK):
        kern[k] = kernel_tile(THICK * me + k, (128, 128))
    load_psi.wait()
    load_tab.wait()

    @pl.when(origin)
    def _():
        for chunk in range(2):
            own_load(chunk).wait()

    pl.semaphore_wait(barrier, len(peers))

    def scatter(chunk):
        start, length = CHUNKS[chunk]
        return pltpu.make_async_remote_copy(
            src_ref=psi.at[:, pl.ds(HALF + start, length)],
            dst_ref=piece(3 - x, chunk),
            send_sem=zs.at[2, chunk], recv_sem=zr.at[chunk],
            device_id=(zh * 4 + 3 - x, me), device_id_type=MESH,
        )

    def up(d, chunk):
        return pltpu.make_async_remote_copy(
            src_ref=piece(x, chunk), dst_ref=piece(x, chunk),
            send_sem=zs.at[0 if d == 1 else 1, chunk], recv_sem=zr.at[chunk],
            device_id=at_z(d), device_id_type=MESH,
        )

    def across(d, chunk):
        return pltpu.make_async_remote_copy(
            src_ref=piece(x, chunk), dst_ref=piece(x, chunk),
            send_sem=xs.at[d - 1, chunk], recv_sem=xr.at[d - 1, chunk],
            device_id=at_x(d), device_id_type=MESH,
        )

    def arrived(chunk):
        up(1, chunk).wait_recv()

    def all_across(chunk):
        for d in (1, 3, 2):
            across(d, chunk).start()

    @pl.when(origin)
    def _():
        for chunk in range(2):
            scatter(chunk).start()

    @pl.when(zh == 0)
    def _():
        for chunk in range(2):
            @pl.when(x >= 2)
            def _():
                arrived(chunk)

            up(1 if chunk == 0 else 3, chunk).start()
            all_across(chunk)
        up(3, 0).start()
        up(1, 1).start()

    @pl.when(zh == 1)
    def _():
        arrived(0)
        up(1, 0).start()
        all_across(0)
        arrived(1)
        all_across(1)

    @pl.when(zh == 3)
    def _():
        arrived(1)
        up(3, 1).start()
        all_across(1)
        arrived(0)
        all_across(0)

    @pl.when(zh == 2)
    def _():
        for chunk in range(2):
            arrived(chunk)
            all_across(chunk)

    for chunk in range(2):
        for d in (1, 2, 3):
            other = (x + 4 - d) % 4
            pltpu.make_async_remote_copy(
                src_ref=piece(x, chunk), dst_ref=piece(other, chunk),
                send_sem=xs.at[d - 1, chunk], recv_sem=xr.at[d - 1, chunk],
                device_id=at_x(d), device_id_type=MESH,
            ).wait_recv()

    field = psi[...]
    for which in range(2):
        density = field * src[which]
        for y in range(NG):
            work[8 * y : 8 * y + THICK, 128 * which : 128 * which + NG] = density[:, NG * y : NG * (y + 1)]
    for part in range(4):
        rows = slice(224 * part, 224 * (part + 1))
        values = from_right(work[rows, :], tab[0], tab[1])
        spec[0, rows, :] = values[:, 0:128]
        spec[1, rows, :] = values[:, 128:256]

    def forward_second(planes):
        columns = []
        for plane in planes:
            columns.append(jnp.concatenate([spec[part, pl.ds(plane, NG, stride=8), :] for part in range(2)], axis=0))
        values = jnp.concatenate(columns, axis=1)
        result = from_left(tab[2, :, 0 : 2 * NG], tab[3, :, 0 : 2 * NG], values)
        for place, plane in enumerate(planes):
            for share in range(SHARES):
                start = BLOCK * share + ROWS * plane
                s_out[start : start + ROWS, :] = result[16 * share : 16 * share + ROWS, 128 * place : 128 * (place + 1)]

    for planes in ((0, 1), (2, 3), (4, 5), (6,)):
        forward_second(planes)

    def block(buffer, share):
        return buffer.at[pl.ds(pl.multiple_of(BLOCK * share, 8), USED)]

    def exchange(source, target, send, receive, d):
        return pltpu.make_async_remote_copy(
            src_ref=block(source, (me + d) % SHARES), dst_ref=block(target, me),
            send_sem=send.at[d - 1], recv_sem=receive.at[d - 1],
            device_id=at_plane(d), device_id_type=MESH,
        )

    def arrival(source, target, send, receive, d):
        return pltpu.make_async_remote_copy(
            src_ref=block(source, me), dst_ref=block(target, (me + SHARES - d) % SHARES),
            send_sem=send.at[d - 1], recv_sem=receive.at[d - 1],
            device_id=at_plane(d), device_id_type=MESH,
        )

    def keep(source, target):
        rows = pl.ds(pl.multiple_of(BLOCK * me, 8), BLOCK)
        target[rows, :] = source[rows, :]

    for d in range(1, SHARES):
        exchange(s_out, r_in, fs, fr, d).start()
    keep(s_out, r_in)
    for which in range(2):
        for y in range(NG):
            srows[which, 8 * y : 8 * y + THICK, 0:NG] = src[which, :, NG * y : NG * (y + 1)]
    for d in range(1, SHARES):
        arrival(s_out, r_in, fs, fr, d).wait_recv()

    def middle(waves):
        columns = []
        for k in waves:
            columns.append(jnp.concatenate(
                [r_in[pl.ds(k, 128, stride=ROWS), :], r_in[pl.ds(THICK + k, 128, stride=ROWS), :]], axis=0))
        spectrum = from_left(tab[4], tab[5], jnp.concatenate(columns, axis=1))
        factor = jnp.concatenate([kern[k] for k in waves], axis=1)
        spectrum = spectrum * jnp.concatenate([factor, factor], axis=0)
        result = from_left(tab[6], tab[7], spectrum)
        for place, k in enumerate(waves):
            lanes = slice(128 * place, 128 * (place + 1))
            g_out[pl.ds(k, 128, stride=ROWS), :] = result[0:128, lanes]
            g_out[pl.ds(THICK + k, 128, stride=ROWS), :] = result[128:256, lanes]

    for waves in ((0, 1), (2, 3), (4, 5), (6,)):
        middle(waves)

    for d in range(1, SHARES):
        exchange(g_out, h_in, bs, br, d).start()
    keep(g_out, h_in)
    for d in range(1, SHARES):
        arrival(g_out, h_in, bs, br, d).wait_recv()

    def back_second(planes):
        columns = []
        for plane in planes:
            columns.append(jnp.concatenate(
                [h_in[BLOCK * q + ROWS * plane : BLOCK * q + ROWS * plane + 16, :] for q in range(SHARES)], axis=0))
        values = from_left(tab[8, 0 : 2 * NG], tab[9, 0 : 2 * NG], jnp.concatenate(columns, axis=1))
        for place, plane in enumerate(planes):
            lanes = slice(128 * place, 128 * (place + 1))
            both = jnp.concatenate([values[0:NG, lanes], values[NG : 2 * NG, lanes]], axis=1)
            potential = from_right(both, tab[10], tab[11])
            rows = pl.ds(plane, NG, stride=8)
            sums[rows, :] = potential[:, 0:128] * srows[0, rows, :] + potential[:, 128:256] * srows[1, rows, :]

    for planes in ((0, 1), (2, 3), (4, 5), (6,)):
        back_second(planes)
    for y in range(NG):
        out[:, NG * y : NG * (y + 1)] = sums[8 * y : 8 * y + THICK, 0:NG]

    @pl.when(origin)
    def _():
        for chunk in range(2):
            scatter(chunk).wait_send()

    @pl.when(zh == 0)
    def _():
        for chunk in range(2):
            up(1, chunk).wait_send()
            up(3, chunk).wait_send()

    @pl.when(zh == 1)
    def _():
        up(1, 0).wait_send()

    @pl.when(zh == 3)
    def _():
        up(3, 1).wait_send()

    for chunk in range(2):
        for d in (1, 2, 3):
            across(d, chunk).wait_send()
    for d in range(1, SHARES):
        exchange(s_out, r_in, fs, fr, d).wait_send()
        exchange(g_out, h_in, bs, br, d).wait_send()


def on_device(orbitals):
    table = jnp.asarray(tables())
    field = orbitals.reshape(THICK, FLAT)
    dma = pltpu.SemaphoreType.DMA
    vmem = pltpu.VMEM
    total = pl.pallas_call(
        body,
        out_shape=jax.ShapeDtypeStruct((THICK, FLAT), f32),
        in_specs=[pl.BlockSpec(memory_space=pl.ANY)] * 2,
        out_specs=pl.BlockSpec(memory_space=vmem),
        scratch_shapes=[
            vmem((THICK, FLAT), f32),
            vmem((12, 256, 256), bf16),
            vmem((2, THICK, FLAT), f32),
            vmem((8 * NG, 256), f32),
            vmem((2, 8 * NG, 128), f32),
            vmem((THICK, 128, 128), f32),
            vmem((SHARES * BLOCK, 128), f32),
            vmem((SHARES * BLOCK, 128), f32),
            vmem((SHARES * BLOCK, 128), f32),
            vmem((SHARES * BLOCK, 128), f32),
            vmem((8 * NG, 128), f32),
            vmem((2, 8 * NG, 128), f32),
            dma((4,)), dma((3, 2)), dma((2,)), dma((3, 2)), dma((3, 2)),
            dma((15,)), dma((15,)), dma((15,)), dma((15,)),
        ],
        compiler_params=pltpu.CompilerParams(collective_id=0, has_side_effects=True),
    )(field, table)
    return total.reshape(orbitals.shape)


def solution(mesh):
    spec = P("band", "plane", None)
    return jax.shard_map(on_device, mesh=mesh, in_specs=(spec,), out_specs=spec, check_vma=False)
```

time: 137 us -> 60.9 us (0.44)
  the two profiles are of different devices: /device:TPU:1 before, /device:TPU:161 now
where the time goes in v1:
time: 60.9 us; the launch traced here: 60.7 us
  Pallas kernels  56.9 us (93%)
  local copies, waits for them, and re-layouts  3.86 us (6%)
    pallas_call x1, Pallas kernels, on_device(): pl.pallas_call(body, out_shape=jax.ShapeDtypeStruct((THICK, FLAT), f32),...  56.9 us
    reshape x1, local copies, waits for them, and re-layouts, on_device(): return total.reshape(orbitals.shape)  2.09 us
    unnamed x1, local copies, waits for them, and re-layouts  1.77 us

profile of v1, /device:TPU:161, one launch (start us, length us, event | category | flops | bytes accessed | tf_op | source)
XLA Modules:
  0.0 60.7 jit_solution(16052251107387759847)
XLA Ops:
  0.0 1.8 %copy.6 = f32[1,7,12544]{2,1,0:T(8,128)} copy(f32[1,7,12544]{2,0,1:T(1,128)} %param.2) | data formatting | bytes 702464
  1.8 56.9 %shard_map.28 = f32[7,12544]{1,0:T(8,128)} custom-call(f32[7,12544]{1,0:T(8,128)} %bitcast.5, bf16[12,256,256]{2,1,0:T(8,128)(2,1)} %constant.2.clone.tab_hbm), custom_call_target="tpu_custom_call" | custom-call | tf_op jit(solution)/shard_map/pallas_call | solution.py:368
  58.7 2.1 %copy.3 = f32[1,7,12544]{2,0,1:T(1,128)} copy(f32[1,7,12544]{2,1,0:T(8,128)} %bitcast.4) | data formatting | bytes 702464 | tf_op jit(solution)/shard_map/reshape | solution.py:391

commit v2 on v1

v2 whole, which is shorter than its diff:
```python
import math

import jax
import jax.numpy as jnp
import ml_dtypes
import numpy as np
from jax import lax
from jax.experimental import pallas as pl
from jax.experimental.pallas import tpu as pltpu
from jax.sharding import PartitionSpec as P

MESH = pl.DeviceIdType.MESH
NG = 112
FLAT = NG * NG
LINES = FLAT // 128
HALF = LINES // 2
LAG = 3
SHARES = 16
THICK = NG // SHARES
ROWS = 2 * THICK
BLOCK = 112
USED = THICK * ROWS
ORDER = (10, 11, 8, 9, 6, 14, 7, 13, 2, 3, 4, 12, 5, 15, 1)
screen_omega = 0.106
cell_length = 46.93
mixing = 0.25
f32, bf16 = jnp.float32, jnp.bfloat16


def tables():
    index = np.arange(NG)
    angle = (index[:, None] * index[None, :] % NG) * (2.0 * math.pi / NG)
    cos, sin = np.cos(angle), np.sin(angle)
    re, im = slice(0, NG), slice(128, 128 + NG)
    last = np.zeros((256, 256))
    last[re, re], last[im, re] = cos, sin
    last[re, im], last[im, im] = -sin, cos
    last_back = np.zeros((256, 256))
    last_back[re, re], last_back[im, re] = cos, -sin
    last_back[re, im], last_back[im, im] = sin, cos
    second = np.zeros((256, 256))
    second_back = np.zeros((256, 256))
    for share in range(SHARES):
        for part in range(2):
            for k in range(THICK):
                row, wave = 16 * share + THICK * part + k, THICK * share + k
                if part == 0:
                    second[row, 0:NG], second[row, NG : 2 * NG] = cos[wave], sin[wave]
                    second_back[0:NG, row], second_back[NG : 2 * NG, row] = cos[wave], sin[wave]
                else:
                    second[row, 0:NG], second[row, NG : 2 * NG] = -sin[wave], cos[wave]
                    second_back[0:NG, row], second_back[NG : 2 * NG, row] = -sin[wave], cos[wave]
    place = 8 * (index // THICK) + index % THICK
    first = np.zeros((256, 256))
    first_back = np.zeros((256, 256))
    first[re, place], first[re, 128 + place] = cos, sin
    first[im, place], first[im, 128 + place] = -sin, cos
    first_back[place, re], first_back[place, im] = cos, -sin
    first_back[128 + place, re], first_back[128 + place, im] = sin, cos
    both = []
    for table in (last, second, first, first_back, second_back, last_back):
        high = table.astype(ml_dtypes.bfloat16)
        both += [high, (table - high.astype(np.float64)).astype(ml_dtypes.bfloat16)]
    return np.stack(both)


def split(values):
    high = values.astype(bf16)
    return high, (values - high.astype(f32)).astype(bf16)


def dot(a, b):
    return jnp.dot(a, b, preferred_element_type=f32)


def from_left(high, low, values):
    big, small = split(values)
    return dot(high, big) + dot(high, small) + dot(low, big)


def from_right(values, high, low):
    big, small = split(values)
    return dot(big, high) + dot(small, high) + dot(big, low)


def kernel_tile(k_second, shape):
    def wave(index):
        return jnp.where(2 * index < NG, index, index - NG).astype(f32)

    first = wave(lax.broadcasted_iota(jnp.int32, shape, 0))
    last = wave(lax.broadcasted_iota(jnp.int32, shape, 1))
    second = wave(jnp.full(shape, k_second, jnp.int32))
    gsquare = (first * first + second * second + last * last) * (2.0 * math.pi / cell_length) ** 2
    safe = jnp.where(gsquare > 0, gsquare, 1.0)
    values = 4.0 * math.pi / safe * (1.0 - jnp.exp(-safe / (4.0 * screen_omega * screen_omega)))
    values = jnp.where(gsquare > 0, values, math.pi / (screen_omega * screen_omega))
    return values * (-mixing / float(NG) ** 3)


def kernel_axes():
    band = lax.axis_index("band")
    return band % 4, band // 4, lax.axis_index("plane")


def send(source, target, send_sem, recv_sem, device):
    return pltpu.make_async_remote_copy(
        src_ref=source, dst_ref=target, send_sem=send_sem, recv_sem=recv_sem,
        device_id=device, device_id_type=MESH,
    )


def spread(psi_hbm, half_hbm, send_sem, recv_sem):
    x, zh, me = kernel_axes()

    def half(i):
        return send(
            psi_hbm.at[pl.ds(LINES * i + HALF, HALF), 0], half_hbm.at[i, pl.ds(0, HALF)],
            send_sem.at[i], recv_sem.at[i], (zh * 4 + 3 - x, me),
        )

    @pl.when(zh == 0)
    def _():
        barrier = pltpu.get_barrier_semaphore()
        pl.semaphore_signal(barrier, inc=1, device_id=(zh * 4 + 3 - x, me), device_id_type=MESH)
        pl.semaphore_wait(barrier, 1)

        @pl.when(x < 2)
        def _():
            for i in range(THICK):
                half(i).start()
            for i in range(THICK):
                half(i).wait_send()

        @pl.when(x >= 2)
        def _():
            for i in range(THICK):
                half(i).wait_recv()


def body(
    psi_hbm, half_hbm, tab_hbm, out,
    psi, tab, src, psi_y, src_y, kern, s_out, r_in, g_out, h_in,
    load_sem, own_sem, zs, zr, xs, xr, fs, fr, bs, br,
):
    x, zh, me = kernel_axes()
    band = zh * 4 + x

    def at_x(d):
        return (zh * 4 + (x + d) % 4, me)

    def at_z(d):
        return (((zh + d) % 4) * 4 + x, me)

    def at_plane(d):
        return (band, (me + d) % SHARES)

    barrier = pltpu.get_barrier_semaphore()
    peers = [at_x(d) for d in (1, 2, 3)] + [at_z(d) for d in (1, 2, 3)]
    peers += [at_plane(d) for d in range(1, SHARES)]
    for peer in peers:
        pl.semaphore_signal(barrier, inc=1, device_id=peer, device_id_type=MESH)

    load_psi = pltpu.make_async_copy(psi_hbm.at[:, 0], psi, load_sem.at[0])
    load_psi.start()
    load_tab = pltpu.make_async_copy(tab_hbm, tab, load_sem.at[1])
    load_tab.start()

    own_source, own_half = ((x + 1) // 2) % 2, x // 2

    def piece(i):
        return src.at[own_source, own_half, i, pl.ds(0, HALF)]

    def own_from_psi(i):
        return pltpu.make_async_copy(psi_hbm.at[pl.ds(LINES * i, HALF), 0], piece(i), own_sem.at[i])

    def own_from_half(i):
        return pltpu.make_async_copy(half_hbm.at[i, pl.ds(0, HALF)], piece(i), own_sem.at[i])

    @pl.when(zh == 0)
    def _():
        @pl.when(x < 2)
        def _():
            for i in range(THICK):
                own_from_psi(i).start()

        @pl.when(x >= 2)
        def _():
            for i in range(THICK):
                own_from_half(i).start()

    lane = lax.broadcasted_iota(jnp.int32, (HALF // 7, 128), 1)

    def to_rows(rows, at):
        flat = [rows(b) for b in range(7)]
        for a in range(8):
            if a == 0:
                value = flat[0]
            else:
                below = flat[a] if a < 7 else jnp.zeros_like(flat[0])
                value = pltpu.roll(jnp.where(lane < 128 - 16 * a, below, flat[a - 1]), 16 * a, 1)
            at(a, value)

    for buffer in (r_in, h_in):
        for share in range(SHARES):
            rows = slice(BLOCK * share + USED, BLOCK * (share + 1))
            buffer[rows, :] = jnp.zeros((BLOCK - USED, 128), f32)
    load_psi.wait()
    for i in range(THICK):
        for h in range(2):
            def put(a, value, i=i, h=h):
                psi_y[pl.ds(NG * i + 56 * h + a, 7, stride=8), :] = value

            to_rows(lambda b, i=i, h=h: psi[pl.ds(LINES * i + HALF * h + b, 7, stride=7), :], put)
    for k in range(THICK):
        kern[k] = kernel_tile(THICK * me + k, (128, 128))
    load_tab.wait()

    @pl.when(zh == 0)
    def _():
        for i in range(THICK):
            own_from_psi(i).wait()

    pl.semaphore_wait(barrier, len(peers))

    def along_z(d, i):
        return send(piece(i), piece(i), zs.at[d - 1, i], zr.at[i], at_z(d))

    def along_x(d, i):
        return send(piece(i), piece(i), xs.at[d - 1, i], xr.at[i], at_x(d))

    def from_origin(act):
        @pl.when(zh == 0)
        def _():
            for i in range(THICK):
                for d in (2, 3, 1) if i < 2 else (3, 1):
                    act(along_z(d, i))

    def passed_on(i, act):
        if i >= 2:
            @pl.when(zh == (1 if i % 2 == 0 else 3))
            def _():
                act(along_z(1 if i % 2 == 0 else 3, i))

    def block(buffer, share, start, count):
        return buffer.at[pl.ds(BLOCK * share + start, count)]

    def exchange(source, target, send_sem, recv_sem, d, i):
        return send(
            block(source, (me + d) % SHARES, ROWS * i, ROWS), block(target, me, ROWS * i, ROWS),
            send_sem, recv_sem, at_plane(d),
        )

    def keep(source, target):
        rows = pl.ds(pl.multiple_of(BLOCK * me, 8), BLOCK)
        target[rows, :] = source[rows, :]

    def forward(i):
        rows = slice(NG * i, NG * (i + 1))
        for j in range(2):
            for h in range(2):
                def put(a, value, j=j, h=h):
                    src_y[j, pl.ds(NG * i + 56 * h + a, 7, stride=8), :] = value

                to_rows(lambda b, j=j, h=h: src[j, h, i, pl.ds(b, 7, stride=7), :], put)
        field = psi_y[rows, :]
        density = jnp.concatenate([field * src_y[0, rows, :], field * src_y[1, rows, :]], axis=1)
        values = from_right(density, tab[0], tab[1])
        values = jnp.concatenate([values[:, 0:128], values[:, 128:256]], axis=0)
        values = from_left(tab[2, :, 0 : 2 * NG], tab[3, :, 0 : 2 * NG], values)
        for share in range(SHARES):
            start = BLOCK * share + ROWS * i
            s_out[start : start + ROWS, :] = values[16 * share : 16 * share + ROWS, :]

    from_origin(lambda copy: copy.start())
    for step in range(THICK + LAG):
        if step < THICK:
            @pl.when(zh != 0)
            def _():
                along_z(1, step).wait_recv()

            passed_on(step, lambda copy: copy.start())
            for d in (1, 3, 2):
                along_x(d, step).start()
        if step >= LAG:
            i = step - LAG
            gone = s_out.at[pl.ds(0, 3 * HALF)]
            send(gone, gone, xs.at[0, i], xr.at[i], at_x(1)).wait_recv()
            forward(i)
            for d in ORDER:
                exchange(s_out, r_in, fs, fr, d, i).start()
    keep(s_out, r_in)
    whole = pl.ds(0, (SHARES - 1) * USED)
    send(s_out.at[whole], r_in.at[whole], fs, fr, at_plane(1)).wait_recv()

    def middle(waves):
        columns = []
        for k in waves:
            columns.append(jnp.concatenate(
                [r_in[pl.ds(k, 128, stride=ROWS), :], r_in[pl.ds(THICK + k, 128, stride=ROWS), :]], axis=0))
        spectrum = from_left(tab[4], tab[5], jnp.concatenate(columns, axis=1))
        factor = jnp.concatenate([kern[k] for k in waves], axis=1)
        spectrum = spectrum * jnp.concatenate([factor, factor], axis=0)
        result = from_left(tab[6], tab[7], spectrum)
        for place, k in enumerate(waves):
            lanes = slice(128 * place, 128 * (place + 1))
            g_out[pl.ds(k, 128, stride=ROWS), :] = result[0:128, lanes]
            g_out[pl.ds(THICK + k, 128, stride=ROWS), :] = result[128:256, lanes]

    for waves in ((0, 1), (2, 3), (4, 5), (6,)):
        middle(waves)

    for i in reversed(range(THICK)):
        for d in ORDER:
            exchange(g_out, h_in, bs, br.at[i], d, i).start()
    keep(g_out, h_in)

    def result(i):
        rows = pl.ds(LINES * i, LINES)
        return pltpu.make_async_copy(psi.at[rows], out.at[rows, 0], own_sem.at[i])

    out_lane = lax.broadcasted_iota(jnp.int32, (NG // 8, 128), 1)

    def back(i):
        columns = [h_in[BLOCK * q + ROWS * i : BLOCK * q + ROWS * i + 16, :] for q in range(SHARES)]
        values = from_left(tab[8, 0 : 2 * NG], tab[9, 0 : 2 * NG], jnp.concatenate(columns, axis=0))
        both = jnp.concatenate([values[0:NG], values[NG : 2 * NG]], axis=1)
        potential = from_right(both, tab[10], tab[11])
        rows = slice(NG * i, NG * (i + 1))
        psi_y[rows, :] = potential[:, 0:128] * src_y[0, rows, :] + potential[:, 128:256] * src_y[1, rows, :]
        turned = []
        for a in range(8):
            value = psi_y[pl.ds(NG * i + a, NG // 8, stride=8), :]
            turned.append(pltpu.roll(value, 128 - 16 * a, 1) if a else value)
        for b in range(7):
            value = jnp.where(out_lane < NG - 16 * b, turned[b], turned[b + 1])
            psi[pl.ds(LINES * i + b, NG // 8, stride=7), :] = value

    for i in reversed(range(THICK)):
        rows = pl.ds(0, (SHARES - 1) * ROWS)
        send(g_out.at[rows], h_in.at[rows], bs, br.at[i], at_plane(1)).wait_recv()
        back(i)
        result(i).start()

    for i in range(THICK):
        result(i).wait()
    from_origin(lambda copy: copy.wait_send())
    for i in range(THICK):
        passed_on(i, lambda copy: copy.wait_send())
        for d in (1, 3, 2):
            along_x(d, i).wait_send()
    send(s_out.at[whole], r_in.at[whole], fs, fr, at_plane(1)).wait_send()
    send(g_out.at[whole], h_in.at[whole], bs, br.at[0], at_plane(1)).wait_send()


def on_device(orbitals):
    table = jnp.asarray(tables())
    field = orbitals.reshape(THICK * LINES, 1, 128)
    dma = pltpu.SemaphoreType.DMA
    vmem = pltpu.VMEM
    anywhere = pl.BlockSpec(memory_space=pl.ANY)
    half = pl.pallas_call(
        spread,
        out_shape=jax.ShapeDtypeStruct((THICK, 56, 128), f32),
        in_specs=[anywhere],
        out_specs=anywhere,
        scratch_shapes=[dma((THICK,)), dma((THICK,))],
        compiler_params=pltpu.CompilerParams(collective_id=1, has_side_effects=True),
    )(field)
    exchanged = vmem((SHARES * BLOCK, 128), f32)
    total = pl.pallas_call(
        body,
        out_shape=jax.ShapeDtypeStruct((THICK * LINES, 1, 128), f32),
        in_specs=[anywhere] * 3,
        out_specs=anywhere,
        scratch_shapes=[
            vmem((THICK * LINES, 128), f32),
            vmem((12, 256, 256), bf16),
            vmem((2, 2, THICK, 56, 128), f32),
            vmem((THICK * NG, 128), f32),
            vmem((2, THICK * NG, 128), f32),
            vmem((THICK, 128, 128), f32),
            exchanged, exchanged, exchanged, exchanged,
            dma((2,)), dma((THICK,)), dma((3, THICK)), dma((THICK,)), dma((3, THICK)), dma((THICK,)),
            dma, dma, dma, dma((THICK,)),
        ],
        compiler_params=pltpu.CompilerParams(collective_id=0, has_side_effects=True),
    )(field, half, table)
    return total.reshape(orbitals.shape)


def solution(mesh):
    spec = P("band", "plane", None)
    return jax.shard_map(on_device, mesh=mesh, in_specs=(spec,), out_specs=spec, check_vma=False)
```

time: 60.9 us -> 52.9 us (0.87)
  the two profiles are of different devices: /device:TPU:161 before, /device:TPU:129 now
where the time goes in v2:
time: 52.9 us; the launch traced here: 52.8 us
  Pallas kernels  51 us (96%)
  local copies, waits for them, and re-layouts  1.74 us (3%)
    pallas_call x1, Pallas kernels, on_device(): pl.pallas_call(body, out_shape=jax.ShapeDtypeStruct((THICK * LINES, 1, 12...  50.9 us
    unnamed x1, local copies, waits for them, and re-layouts  1.74 us

profile of v2, /device:TPU:129, one launch (start us, length us, event | category | flops | bytes accessed | tf_op | source)
XLA Modules:
  0.0 52.8 jit_solution(1857391299083853512)
XLA Ops:
  0.0 0.1 shard_map.28.half_hbm
  0.1 50.9 %shard_map.29 = f32[686,1,128]{2,1,0:T(1,128)} custom-call(f32[686,1,128]{2,1,0:T(1,128)} %bitcast.3, f32[7,56,128]{2,1,0:T(8,128)} %shard_map.28.half_hbm, bf16[12,256,256]{2,1,0:T(8,128)(2,1)} %constant.2.clone.tab_hbm), custom_call_target="tpu_custom_call" | custom-call | tf_op jit(solution)/shard_map/pallas_call | solution.py:370
  51.0 1.7 %copy.6 = f32[1,7,12544]{2,0,1:T(1,128)} copy(f32[1,7,12544]{2,0,1:T(1,128)} %bitcast.4) | data formatting | bytes 702464

commit v3 on v2

--- a/solution.py
+++ b/solution.py
@@ -14,7 +14,8 @@
 FLAT = NG * NG
 LINES = FLAT // 128
 HALF = LINES // 2
-LAG = 3
+EVEN_FIRST = (-1, -3, -5, -7, 1, 3, -2, 5, -4, 7, -6, 2, 4, 6)
+ODD_FIRST = (-2, -4, -1, -6, -3, 2, -5, 4, -7, 1, 6, 3, 5, 7)
 SHARES = 16
 THICK = NG // SHARES
 ROWS = 2 * THICK
@@ -231,15 +232,19 @@
     def from_origin(act):
         @pl.when(zh == 0)
         def _():
-            for i in range(THICK):
-                for d in (2, 3, 1) if i < 2 else (3, 1):
+            for i in (0, 2, 4, 6):
+                act(along_z(2, i))
+            for i in (1, 3, 5):
+                for d in (3, 1):
                     act(along_z(d, i))
 
     def passed_on(i, act):
-        if i >= 2:
-            @pl.when(zh == (1 if i % 2 == 0 else 3))
-            def _():
-                act(along_z(1 if i % 2 == 0 else 3, i))
+        relay = 2 if i % 2 == 0 else 3 if i == 3 else 1
+
+        @pl.when(zh == relay)
+        def _():
+            for d in (1, 3) if relay == 2 else (relay,):
+                act(along_z(d, i))
 
     def block(buffer, share, start, count):
         return buffer.at[pl.ds(BLOCK * share + start, count)]
@@ -272,22 +277,35 @@
             s_out[start : start + ROWS, :] = values[16 * share : 16 * share + ROWS, :]
 
     from_origin(lambda copy: copy.start())
-    for step in range(THICK + LAG):
-        if step < THICK:
-            @pl.when(zh != 0)
-            def _():
-                along_z(1, step).wait_recv()
-
-            passed_on(step, lambda copy: copy.start())
-            for d in (1, 3, 2):
-                along_x(d, step).start()
-        if step >= LAG:
-            i = step - LAG
-            gone = s_out.at[pl.ds(0, 3 * HALF)]
-            send(gone, gone, xs.at[0, i], xr.at[i], at_x(1)).wait_recv()
-            forward(i)
-            for d in ORDER:
-                exchange(s_out, r_in, fs, fr, d, i).start()
+
+    def pass_on(i):
+        @pl.when(zh != 0)
+        def _():
+            along_z(1, i).wait_recv()
+
+        passed_on(i, lambda copy: copy.start())
+        for d in (1, 3, 2):
+            along_x(d, i).start()
+
+    def take(i):
+        gone = s_out.at[pl.ds(0, 3 * HALF)]
+        send(gone, gone, xs.at[0, i], xr.at[i], at_x(1)).wait_recv()
+        forward(i)
+        for d in ORDER:
+            exchange(s_out, r_in, fs, fr, d, i).start()
+
+    def in_order(steps):
+        for step in steps:
+            (pass_on if step < 0 else take)(abs(step) - 1)
+
+    @pl.when(zh == 2)
+    def _():
+        in_order(EVEN_FIRST)
+
+    @pl.when(zh != 2)
+    def _():
+        in_order(ODD_FIRST)
+
     keep(s_out, r_in)
     whole = pl.ds(0, (SHARES - 1) * USED)
     send(s_out.at[whole], r_in.at[whole], fs, fr, at_plane(1)).wait_recv()

time: 52.9 us -> 50.4 us (0.953)
  the two profiles are of different devices: /device:TPU:129 before, /device:TPU:65 now
where the time goes in v3:
time: 50.4 us; the launch traced here: 50.3 us
  Pallas kernels  48.5 us (96%)
  local copies, waits for them, and re-layouts  1.74 us (3%)
    pallas_call x1, Pallas kernels, on_device(): pl.pallas_call(body, out_shape=jax.ShapeDtypeStruct((THICK * LINES, 1, 12...  48.4 us
    unnamed x1, local copies, waits for them, and re-layouts  1.74 us

profile of v3, /device:TPU:65, one launch (start us, length us, event | category | flops | bytes accessed | tf_op | source)
XLA Modules:
  0.0 50.3 jit_solution(4294767422283773280)
XLA Ops:
  0.0 0.1 shard_map.28.half_hbm
  0.1 48.4 %shard_map.29 = f32[686,1,128]{2,1,0:T(1,128)} custom-call(f32[686,1,128]{2,1,0:T(1,128)} %bitcast.3, f32[7,56,128]{2,1,0:T(8,128)} %shard_map.28.half_hbm, bf16[12,256,256]{2,1,0:T(8,128)(2,1)} %constant.2.clone.tab_hbm), custom_call_target="tpu_custom_call" | custom-call | tf_op jit(solution)/shard_map/pallas_call | solution.py:388
  48.6 1.7 %copy.6 = f32[1,7,12544]{2,0,1:T(1,128)} copy(f32[1,7,12544]{2,0,1:T(1,128)} %bitcast.4) | data formatting | bytes 702464

commit v4 on v3

--- a/solution.py
+++ b/solution.py
@@ -201,6 +201,37 @@
                 value = pltpu.roll(jnp.where(lane < 128 - 16 * a, below, flat[a - 1]), 16 * a, 1)
             at(a, value)
 
+    def along_z(d, i):
+        return send(piece(i), piece(i), zs.at[d - 1, i], zr.at[i], at_z(d))
+
+    def along_x(d, i):
+        return send(piece(i), piece(i), xs.at[d - 1, i], xr.at[i], at_x(d))
+
+    def from_origin(act):
+        @pl.when(zh == 0)
+        def _():
+            for i in (0, 2, 4, 6):
+                act(along_z(2, i))
+            for i in (1, 3, 5):
+                for d in (3, 1):
+                    act(along_z(d, i))
+
+    def passed_on(i, act):
+        relay = 2 if i % 2 == 0 else 3 if i == 3 else 1
+
+        @pl.when(zh == relay)
+        def _():
+            for d in (1, 3) if relay == 2 else (relay,):
+                act(along_z(d, i))
+
+    @pl.when(zh == 0)
+    def _():
+        for i in range(THICK):
+            own_from_psi(i).wait()
+        pl.semaphore_wait(barrier, len(peers))
+
+    from_origin(lambda copy: copy.start())
+
     for buffer in (r_in, h_in):
         for share in range(SHARES):
             rows = slice(BLOCK * share + USED, BLOCK * (share + 1))
@@ -216,35 +247,9 @@
         kern[k] = kernel_tile(THICK * me + k, (128, 128))
     load_tab.wait()
 
-    @pl.when(zh == 0)
-    def _():
-        for i in range(THICK):
-            own_from_psi(i).wait()
-
-    pl.semaphore_wait(barrier, len(peers))
-
-    def along_z(d, i):
-        return send(piece(i), piece(i), zs.at[d - 1, i], zr.at[i], at_z(d))
-
-    def along_x(d, i):
-        return send(piece(i), piece(i), xs.at[d - 1, i], xr.at[i], at_x(d))
-
-    def from_origin(act):
-        @pl.when(zh == 0)
-        def _():
-            for i in (0, 2, 4, 6):
-                act(along_z(2, i))
-            for i in (1, 3, 5):
-                for d in (3, 1):
-                    act(along_z(d, i))
-
-    def passed_on(i, act):
-        relay = 2 if i % 2 == 0 else 3 if i == 3 else 1
-
-        @pl.when(zh == relay)
-        def _():
-            for d in (1, 3) if relay == 2 else (relay,):
-                act(along_z(d, i))
+    @pl.when(zh != 0)
+    def _():
+        pl.semaphore_wait(barrier, len(peers))
 
     def block(buffer, share, start, count):
         return buffer.at[pl.ds(BLOCK * share + start, count)]
@@ -275,8 +280,6 @@
         for share in range(SHARES):
             start = BLOCK * share + ROWS * i
             s_out[start : start + ROWS, :] = values[16 * share : 16 * share + ROWS, :]
-
-    from_origin(lambda copy: copy.start())
 
     def pass_on(i):
         @pl.when(zh != 0)
@@ -351,16 +354,13 @@
             turned.append(pltpu.roll(value, 128 - 16 * a, 1) if a else value)
         for b in range(7):
             value = jnp.where(out_lane < NG - 16 * b, turned[b], turned[b + 1])
-            psi[pl.ds(LINES * i + b, NG // 8, stride=7), :] = value
+            out[pl.ds(LINES * i + b, NG // 8, stride=7), 0, :] = value
 
     for i in reversed(range(THICK)):
         rows = pl.ds(0, (SHARES - 1) * ROWS)
         send(g_out.at[rows], h_in.at[rows], bs, br.at[i], at_plane(1)).wait_recv()
         back(i)
-        result(i).start()
-
-    for i in range(THICK):
-        result(i).wait()
+
     from_origin(lambda copy: copy.wait_send())
     for i in range(THICK):
         passed_on(i, lambda copy: copy.wait_send())
@@ -387,9 +387,9 @@
     exchanged = vmem((SHARES * BLOCK, 128), f32)
     total = pl.pallas_call(
         body,
-        out_shape=jax.ShapeDtypeStruct((THICK * LINES, 1, 128), f32),
+        out_shape=pltpu.VMEM((THICK * LINES, 1, 128), f32),
         in_specs=[anywhere] * 3,
-        out_specs=anywhere,
+        out_specs=pl.BlockSpec(memory_space=vmem),
         scratch_shapes=[
             vmem((THICK * LINES, 128), f32),
             vmem((12, 256, 256), bf16),

time: 50.4 us -> 48.8 us (0.968)
  local copies, waits for them, and re-layouts: 1.74 us -> 0.73 us
  Pallas kernels: 48.5 us -> 47.9 us
    unnamed x1, local copies, waits for them, and re-layouts: 1.74 us -> 0.73 us
    pallas_call x1, Pallas kernels: 48.4 us -> 47.8 us  [on_device(): pl.pallas_call(body, out_shape=pltpu.VMEM((THICK * LINES, 1, 128), f32),...]
where the time goes in v4:
time: 48.8 us; the launch traced here: 48.7 us
  Pallas kernels  47.9 us (98%)
  local copies, waits for them, and re-layouts  0.73 us (1%)
    pallas_call x1, Pallas kernels, on_device(): pl.pallas_call(body, out_shape=pltpu.VMEM((THICK * LINES, 1, 128), f32),...  47.8 us

profile of v4, /device:TPU:65, one launch (start us, length us, event | category | flops | bytes accessed | tf_op | source)
XLA Modules:
  0.0 48.7 jit_solution(7152189449430687880)
XLA Ops:
  0.0 0.1 shard_map.28.half_hbm
  0.1 47.8 %shard_map.29 = f32[686,1,128]{2,1,0:T(1,128)S(1)} custom-call(f32[686,1,128]{2,1,0:T(1,128)} %bitcast.4, f32[7,56,128]{2,1,0:T(8,128)} %shard_map.28.half_hbm, bf16[12,256,256]{2,1,0:T(8,128)(2,1)} %constant.2.clone.tab_hbm), custom_call_target="tpu_custom_call" | custom-call | tf_op jit(solution)/shard_map/pallas_call | solution.py:388
  48.0 0.7 %copy.6 = f32[1,7,12544]{2,0,1:T(1,128)} copy(f32[1,7,12544]{2,0,1:T(1,128)S(1)} %bitcast.2) | data formatting | bytes 702464

commit v5 on v4

--- a/solution.py
+++ b/solution.py
@@ -152,8 +152,12 @@
     def at_z(d):
         return (((zh + d) % 4) * 4 + x, me)
 
+    def share_of(d):
+        y, z, c = me // 4, (me // 2) % 2, me % 2
+        return ((y + d // 4) % 4) * 4 + ((z + (d // 2) % 2) % 2) * 2 + (c + d % 2) % 2
+
     def at_plane(d):
-        return (band, (me + d) % SHARES)
+        return (band, share_of(d))
 
     barrier = pltpu.get_barrier_semaphore()
     peers = [at_x(d) for d in (1, 2, 3)] + [at_z(d) for d in (1, 2, 3)]
@@ -256,7 +260,7 @@
 
     def exchange(source, target, send_sem, recv_sem, d, i):
         return send(
-            block(source, (me + d) % SHARES, ROWS * i, ROWS), block(target, me, ROWS * i, ROWS),
+            block(source, share_of(d), ROWS * i, ROWS), block(target, me, ROWS * i, ROWS),
             send_sem, recv_sem, at_plane(d),
         )
 
@@ -313,22 +317,26 @@
     whole = pl.ds(0, (SHARES - 1) * USED)
     send(s_out.at[whole], r_in.at[whole], fs, fr, at_plane(1)).wait_recv()
 
-    def middle(waves):
+    def first_part(waves):
         columns = []
         for k in waves:
             columns.append(jnp.concatenate(
                 [r_in[pl.ds(k, 128, stride=ROWS), :], r_in[pl.ds(THICK + k, 128, stride=ROWS), :]], axis=0))
         spectrum = from_left(tab[4], tab[5], jnp.concatenate(columns, axis=1))
         factor = jnp.concatenate([kern[k] for k in waves], axis=1)
-        spectrum = spectrum * jnp.concatenate([factor, factor], axis=0)
+        return spectrum * jnp.concatenate([factor, factor], axis=0)
+
+    def second_part(waves, spectrum):
         result = from_left(tab[6], tab[7], spectrum)
         for place, k in enumerate(waves):
             lanes = slice(128 * place, 128 * (place + 1))
             g_out[pl.ds(k, 128, stride=ROWS), :] = result[0:128, lanes]
             g_out[pl.ds(THICK + k, 128, stride=ROWS), :] = result[128:256, lanes]
 
-    for waves in ((0, 1), (2, 3), (4, 5), (6,)):
-        middle(waves)
+    groups = ((0, 1), (2, 3), (4, 5), (6,))
+    held = [first_part(waves) for waves in groups]
+    for waves, spectrum in zip(groups, held):
+        second_part(waves, spectrum)
 
     for i in reversed(range(THICK)):
         for d in ORDER:

time: 48.8 us -> 47.9 us (0.982)
  Pallas kernels: 47.9 us -> 47.1 us
    pallas_call x1, Pallas kernels: 47.8 us -> 46.9 us  [on_device(): pl.pallas_call(body, out_shape=pltpu.VMEM((THICK * LINES, 1, 128), f32),...]
where the time goes in v5:
time: 47.9 us; the launch traced here: 47.8 us
  Pallas kernels  47.1 us (98%)
  local copies, waits for them, and re-layouts  0.73 us (2%)
    pallas_call x1, Pallas kernels, on_device(): pl.pallas_call(body, out_shape=pltpu.VMEM((THICK * LINES, 1, 128), f32),...  46.9 us

profile of v5, /device:TPU:65, one launch (start us, length us, event | category | flops | bytes accessed | tf_op | source)
XLA Modules:
  0.0 47.8 jit_solution(2116600499677002984)
XLA Ops:
  0.0 0.1 shard_map.28.half_hbm
  0.1 46.9 %shard_map.29 = f32[686,1,128]{2,1,0:T(1,128)S(1)} custom-call(f32[686,1,128]{2,1,0:T(1,128)} %bitcast.4, f32[7,56,128]{2,1,0:T(8,128)} %shard_map.28.half_hbm, bf16[12,256,256]{2,1,0:T(8,128)(2,1)} %constant.2.clone.tab_hbm), custom_call_target="tpu_custom_call" | custom-call | tf_op jit(solution)/shard_map/pallas_call | solution.py:396
  47.1 0.7 %copy.6 = f32[1,7,12544]{2,0,1:T(1,128)} copy(f32[1,7,12544]{2,0,1:T(1,128)S(1)} %bitcast.2) | data formatting | bytes 702464

commit v6 on v5

--- a/solution.py
+++ b/solution.py
@@ -14,12 +14,13 @@
 FLAT = NG * NG
 LINES = FLAT // 128
 HALF = LINES // 2
-EVEN_FIRST = (-1, -3, -5, -7, 1, 3, -2, 5, -4, 7, -6, 2, 4, 6)
-ODD_FIRST = (-2, -4, -1, -6, -3, 2, -5, 4, -7, 1, 6, 3, 5, 7)
+EVEN_FIRST = (-1, -3, -5, 1, 3, -2, 5, -4, -6, 2, -7, 4, 6, 7)
+ODD_FIRST = (-2, -4, -6, -1, 2, -7, -3, 4, -5, 6, 1, 7, 3, 5)
 SHARES = 16
 THICK = NG // SHARES
 ROWS = 2 * THICK
 BLOCK = 112
+SENT = ROWS - 1
 USED = THICK * ROWS
 ORDER = (10, 11, 8, 9, 6, 14, 7, 13, 2, 3, 4, 12, 5, 15, 1)
 screen_omega = 0.106
@@ -214,14 +215,14 @@
     def from_origin(act):
         @pl.when(zh == 0)
         def _():
-            for i in (0, 2, 4, 6):
+            for i in (0, 2, 4):
                 act(along_z(2, i))
-            for i in (1, 3, 5):
+            for i in (1, 3, 5, 6):
                 for d in (3, 1):
                     act(along_z(d, i))
 
     def passed_on(i, act):
-        relay = 2 if i % 2 == 0 else 3 if i == 3 else 1
+        relay = (2, 1, 2, 3, 2, 1, 3)[i]
 
         @pl.when(zh == relay)
         def _():
@@ -258,15 +259,29 @@
     def block(buffer, share, start, count):
         return buffer.at[pl.ds(BLOCK * share + start, count)]
 
-    def exchange(source, target, send_sem, recv_sem, d, i):
+    def exchange(source, target, send_sem, recv_sem, d, i, rows=ROWS):
         return send(
-            block(source, share_of(d), ROWS * i, ROWS), block(target, me, ROWS * i, ROWS),
+            block(source, share_of(d), ROWS * i, rows), block(target, me, ROWS * i, rows),
             send_sem, recv_sem, at_plane(d),
         )
 
     def keep(source, target):
         rows = pl.ds(pl.multiple_of(BLOCK * me, 8), BLOCK)
         target[rows, :] = source[rows, :]
+
+    def of_all(i, row):
+        return pl.ds(ROWS * i + row, SHARES, stride=BLOCK)
+
+    def tucked(row, last, g):
+        lanes = lax.broadcasted_iota(jnp.int32, row.shape, 1)
+        return jnp.where(lanes < NG, row, pltpu.roll(last, NG - 16 * g, 1))
+
+    def untucked(row):
+        last = pltpu.roll(row(0), 16, 1)
+        lanes = lax.broadcasted_iota(jnp.int32, last.shape, 1)
+        for g in range(1, 7):
+            last = jnp.where(lanes < 16 * g, last, pltpu.roll(row(g), 16 + 16 * g, 1))
+        return last
 
     def forward(i):
         rows = slice(NG * i, NG * (i + 1))
@@ -315,32 +330,39 @@
 
     keep(s_out, r_in)
     whole = pl.ds(0, (SHARES - 1) * USED)
+    packed = pl.ds(0, (SHARES - 1) * THICK * SENT)
     send(s_out.at[whole], r_in.at[whole], fs, fr, at_plane(1)).wait_recv()
 
     def first_part(waves):
         columns = []
         for k in waves:
-            columns.append(jnp.concatenate(
-                [r_in[pl.ds(k, 128, stride=ROWS), :], r_in[pl.ds(THICK + k, 128, stride=ROWS), :]], axis=0))
+            def row(t):
+                return r_in[pl.ds(t, 128, stride=ROWS), :]
+
+            columns.append(jnp.concatenate([row(k), row(THICK + k)], axis=0))
         spectrum = from_left(tab[4], tab[5], jnp.concatenate(columns, axis=1))
         factor = jnp.concatenate([kern[k] for k in waves], axis=1)
         return spectrum * jnp.concatenate([factor, factor], axis=0)
 
-    def second_part(waves, spectrum):
+    def second_part(waves, spectrum, last):
         result = from_left(tab[6], tab[7], spectrum)
+        if last is None:
+            last = result[128:256]
         for place, k in enumerate(waves):
             lanes = slice(128 * place, 128 * (place + 1))
-            g_out[pl.ds(k, 128, stride=ROWS), :] = result[0:128, lanes]
+            g_out[pl.ds(k, 128, stride=ROWS), :] = tucked(result[0:128, lanes], last, k)
             g_out[pl.ds(THICK + k, 128, stride=ROWS), :] = result[128:256, lanes]
+        return last
 
     groups = ((0, 1), (2, 3), (4, 5), (6,))
     held = [first_part(waves) for waves in groups]
-    for waves, spectrum in zip(groups, held):
-        second_part(waves, spectrum)
+    last = None
+    for waves, spectrum in zip(groups[::-1], held[::-1]):
+        last = second_part(waves, spectrum, last)
 
     for i in reversed(range(THICK)):
         for d in ORDER:
-            exchange(g_out, h_in, bs, br.at[i], d, i).start()
+            exchange(g_out, h_in, bs, br.at[i], d, i, SENT).start()
     keep(g_out, h_in)
 
     def result(i):
@@ -350,6 +372,7 @@
     out_lane = lax.broadcasted_iota(jnp.int32, (NG // 8, 128), 1)
 
     def back(i):
+        h_in[of_all(i, SENT), :] = untucked(lambda g: h_in[of_all(i, g), :])
         columns = [h_in[BLOCK * q + ROWS * i : BLOCK * q + ROWS * i + 16, :] for q in range(SHARES)]
         values = from_left(tab[8, 0 : 2 * NG], tab[9, 0 : 2 * NG], jnp.concatenate(columns, axis=0))
         both = jnp.concatenate([values[0:NG], values[NG : 2 * NG]], axis=1)
@@ -365,7 +388,7 @@
             out[pl.ds(LINES * i + b, NG // 8, stride=7), 0, :] = value
 
     for i in reversed(range(THICK)):
-        rows = pl.ds(0, (SHARES - 1) * ROWS)
+        rows = pl.ds(0, (SHARES - 1) * SENT)
         send(g_out.at[rows], h_in.at[rows], bs, br.at[i], at_plane(1)).wait_recv()
         back(i)
 
@@ -375,7 +398,7 @@
         for d in (1, 3, 2):
             along_x(d, i).wait_send()
     send(s_out.at[whole], r_in.at[whole], fs, fr, at_plane(1)).wait_send()
-    send(g_out.at[whole], h_in.at[whole], bs, br.at[0], at_plane(1)).wait_send()
+    send(g_out.at[packed], h_in.at[packed], bs, br.at[0], at_plane(1)).wait_send()
 
 
 def on_device(orbitals):

time: 47.9 us -> 47.4 us (0.990)
  Pallas kernels: 47.1 us -> 46.1 us
    pallas_call x1, Pallas kernels: 46.9 us -> 46 us  [on_device(): pl.pallas_call(body, out_shape=pltpu.VMEM((THICK * LINES, 1, 128), f32),...]
where the time goes in v6:
time: 47.4 us; the launch traced here: 46.9 us
  Pallas kernels  46.1 us (97%)
  local copies, waits for them, and re-layouts  0.73 us (2%)
    pallas_call x1, Pallas kernels, on_device(): pl.pallas_call(body, out_shape=pltpu.VMEM((THICK * LINES, 1, 128), f32),...  46 us

profile of v6, /device:TPU:65, one launch (start us, length us, event | category | flops | bytes accessed | tf_op | source)
XLA Modules:
  0.0 46.9 jit_solution(16517266300754324758)
XLA Ops:
  0.0 0.1 shard_map.28.half_hbm
  0.1 46.0 %shard_map.29 = f32[686,1,128]{2,1,0:T(1,128)S(1)} custom-call(f32[686,1,128]{2,1,0:T(1,128)} %bitcast.4, f32[7,56,128]{2,1,0:T(8,128)} %shard_map.28.half_hbm, bf16[12,256,256]{2,1,0:T(8,128)(2,1)} %constant.2.clone.tab_hbm), custom_call_target="tpu_custom_call" | custom-call | tf_op jit(solution)/shard_map/pallas_call | solution.py:419
  46.2 0.7 %copy.6 = f32[1,7,12544]{2,0,1:T(1,128)} copy(f32[1,7,12544]{2,0,1:T(1,128)S(1)} %bitcast.2) | data formatting | bytes 702464

commit v7 on v6

--- a/solution.py
+++ b/solution.py
@@ -56,9 +56,10 @@
     first = np.zeros((256, 256))
     first_back = np.zeros((256, 256))
     first[re, place], first[re, 128 + place] = cos, sin
-    first[im, place], first[im, 128 + place] = -sin, cos
-    first_back[place, re], first_back[place, im] = cos, -sin
-    first_back[128 + place, re], first_back[128 + place, im] = sin, cos
+    tail = slice(NG, 2 * NG)
+    first[tail, place], first[tail, 128 + place] = -sin, cos
+    first_back[place, re], first_back[place, tail] = cos, -sin
+    first_back[128 + place, re], first_back[128 + place, tail] = sin, cos
     both = []
     for table in (last, second, first, first_back, second_back, last_back):
         high = table.astype(ml_dtypes.bfloat16)
@@ -340,12 +341,12 @@
                 return r_in[pl.ds(t, 128, stride=ROWS), :]
 
             columns.append(jnp.concatenate([row(k), row(THICK + k)], axis=0))
-        spectrum = from_left(tab[4], tab[5], jnp.concatenate(columns, axis=1))
-        factor = jnp.concatenate([kern[k] for k in waves], axis=1)
+        spectrum = from_left(tab[4, 0 : 2 * NG], tab[5, 0 : 2 * NG], jnp.concatenate(columns, axis=1))
+        factor = jnp.concatenate([kern[k, 0:NG] for k in waves], axis=1)
         return spectrum * jnp.concatenate([factor, factor], axis=0)
 
     def second_part(waves, spectrum, last):
-        result = from_left(tab[6], tab[7], spectrum)
+        result = from_left(tab[6, :, 0 : 2 * NG], tab[7, :, 0 : 2 * NG], spectrum)
         if last is None:
             last = result[128:256]
         for place, k in enumerate(waves):

time: 47.4 us -> 47.3 us (level)
  no operation moved by 1% of the time
where the time goes in v7:
time: 47.3 us; the launch traced here: 46.8 us
  Pallas kernels  46.1 us (97%)
  local copies, waits for them, and re-layouts  0.73 us (2%)
    pallas_call x1, Pallas kernels, on_device(): pl.pallas_call(body, out_shape=pltpu.VMEM((THICK * LINES, 1, 128), f32),...  46 us

profile of v7, /device:TPU:65, one launch (start us, length us, event | category | flops | bytes accessed | tf_op | source)
XLA Modules:
  0.0 46.8 jit_solution(4697850020764313212)
XLA Ops:
  0.0 0.1 shard_map.28.half_hbm
  0.1 46.0 %shard_map.29 = f32[686,1,128]{2,1,0:T(1,128)S(1)} custom-call(f32[686,1,128]{2,1,0:T(1,128)} %bitcast.4, f32[7,56,128]{2,1,0:T(8,128)} %shard_map.28.half_hbm, bf16[12,256,256]{2,1,0:T(8,128)(2,1)} %constant.2.clone.tab_hbm), custom_call_target="tpu_custom_call" | custom-call | tf_op jit(solution)/shard_map/pallas_call | solution.py:420
  46.1 0.7 %copy.6 = f32[1,7,12544]{2,0,1:T(1,128)} copy(f32[1,7,12544]{2,0,1:T(1,128)S(1)} %bitcast.2) | data formatting | bytes 702464

commit v8 on v7

--- a/solution.py
+++ b/solution.py
@@ -23,6 +23,7 @@
 SENT = ROWS - 1
 USED = THICK * ROWS
 ORDER = (10, 11, 8, 9, 6, 14, 7, 13, 2, 3, 4, 12, 5, 15, 1)
+CROSSING_FIRST = (10, 11, 2, 3, 6, 14, 7, 15, 8, 9, 4, 12, 5, 13, 1)
 screen_omega = 0.106
 cell_length = 46.93
 mixing = 0.25
@@ -314,7 +315,7 @@
         gone = s_out.at[pl.ds(0, 3 * HALF)]
         send(gone, gone, xs.at[0, i], xr.at[i], at_x(1)).wait_recv()
         forward(i)
-        for d in ORDER:
+        for d in CROSSING_FIRST:
             exchange(s_out, r_in, fs, fr, d, i).start()
 
     def in_order(steps):

time: 47.3 us -> 47.4 us (level)
  no operation moved by 1% of the time
where the time goes in v8:
time: 47.4 us; the launch traced here: 46.9 us
  Pallas kernels  46.1 us (97%)
  local copies, waits for them, and re-layouts  0.73 us (2%)
    pallas_call x1, Pallas kernels, on_device(): pl.pallas_call(body, out_shape=pltpu.VMEM((THICK * LINES, 1, 128), f32),...  46 us

profile of v8, /device:TPU:65, one launch (start us, length us, event | category | flops | bytes accessed | tf_op | source)
XLA Modules:
  0.0 46.9 jit_solution(758927574008891386)
XLA Ops:
  0.0 0.1 shard_map.28.half_hbm
  0.1 46.0 %shard_map.29 = f32[686,1,128]{2,1,0:T(1,128)S(1)} custom-call(f32[686,1,128]{2,1,0:T(1,128)} %bitcast.4, f32[7,56,128]{2,1,0:T(8,128)} %shard_map.28.half_hbm, bf16[12,256,256]{2,1,0:T(8,128)(2,1)} %constant.2.clone.tab_hbm), custom_call_target="tpu_custom_call" | custom-call | tf_op jit(solution)/shard_map/pallas_call | solution.py:421
  46.1 0.7 %copy.6 = f32[1,7,12544]{2,0,1:T(1,128)} copy(f32[1,7,12544]{2,0,1:T(1,128)S(1)} %bitcast.2) | data formatting | bytes 702464

commit v9 on v7

--- a/solution.py
+++ b/solution.py
@@ -307,7 +307,7 @@
             along_z(1, i).wait_recv()
 
         passed_on(i, lambda copy: copy.start())
-        for d in (1, 3, 2):
+        for d in (2, 1, 3):
             along_x(d, i).start()
 
     def take(i):
@@ -396,7 +396,7 @@
     from_origin(lambda copy: copy.wait_send())
     for i in range(THICK):
         passed_on(i, lambda copy: copy.wait_send())
-        for d in (1, 3, 2):
+        for d in (2, 1, 3):
             along_x(d, i).wait_send()
     send(s_out.at[whole], r_in.at[whole], fs, fr, at_plane(1)).wait_send()
     send(g_out.at[packed], h_in.at[packed], bs, br.at[0], at_plane(1)).wait_send()

time: 47.3 us -> 47.4 us (level)
  no operation moved by 1% of the time
where the time goes in v9:
time: 47.4 us; the launch traced here: 47.2 us
  Pallas kernels  46.4 us (98%)
  local copies, waits for them, and re-layouts  0.73 us (2%)
    pallas_call x1, Pallas kernels, on_device(): pl.pallas_call(body, out_shape=pltpu.VMEM((THICK * LINES, 1, 128), f32),...  46.3 us

profile of v9, /device:TPU:65, one launch (start us, length us, event | category | flops | bytes accessed | tf_op | source)
XLA Modules:
  0.0 47.2 jit_solution(17134079059609804128)
XLA Ops:
  0.0 0.1 shard_map.28.half_hbm
  0.1 46.3 %shard_map.29 = f32[686,1,128]{2,1,0:T(1,128)S(1)} custom-call(f32[686,1,128]{2,1,0:T(1,128)} %bitcast.4, f32[7,56,128]{2,1,0:T(8,128)} %shard_map.28.half_hbm, bf16[12,256,256]{2,1,0:T(8,128)(2,1)} %constant.2.clone.tab_hbm), custom_call_target="tpu_custom_call" | custom-call | tf_op jit(solution)/shard_map/pallas_call | solution.py:420
  46.4 0.7 %copy.6 = f32[1,7,12544]{2,0,1:T(1,128)} copy(f32[1,7,12544]{2,0,1:T(1,128)S(1)} %bitcast.2) | data formatting | bytes 702464
